TPU v7x, 32 devices: a whole 2x2x4 slice. The times are simulated.
32 devices in a mesh: pair: 2 (over core), row: 16 (over z, y, x).
Axes of the slice: x: 2, y: 2, z: 4, core: 2. Of those that a mesh axis runs over, the one named last changes fastest.
Arguments:
- snapshot: float32 [4096, 1024], P('row', 'pair'), may hold values from -6 to 6
- weights: float32 [8, 128], replicated, may hold values from 0 to 1
- block_home: int32 [8], P('pair'), may hold values from 0 to 7, each once
- plan: int32 [2, 2, 4], P(None, 'pair'), may hold values from 0 to 3, each once within a row
Outputs:
- rotated: float32 [4096, 1024], P('row', 'pair')
- column_norms: float32 [1024], P('pair')
All inputs are finite; a program needn't handle non-finite values. Where the computation divides by a largest or mean magnitude, that divisor is 1e-20 or more.
Results may differ from a plain program's by a relative error of at most 0.0001.
Values sent between devices are 32-bit elements; how exact they have to be, the bound alone decides.
No kernel may reach another device: no remote copies, remote signals or barrier semaphores. Data moves between devices by JAX's collectives and lax.ppermute only.
A program may use at most 128 MiB of HBM per device.

v0:
```python
import jax
import jax.numpy as jnp
from jax import lax
from jax.sharding import PartitionSpec as P

epsilon = 1e-06
step_size = 4.0
newton_turns = 5
highest = lax.Precision.HIGHEST


def shifted(block, axis, distance):
    devices = range(lax.axis_size(axis))
    route = [((i - distance) % len(devices), i) for i in devices]
    return lax.ppermute(block, axis, route)


def rotation(gram_matrix, spread):
    diagonal_part = jnp.diagonal(gram_matrix, axis1=1, axis2=2)
    inverse = lax.rsqrt(diagonal_part + epsilon)
    corr = gram_matrix * inverse[:, :, None] * inverse[:, None, :]
    skew_part = step_size * corr * (spread[:, :, None] - spread[:, None, :])
    row_bound = 1.0 + jnp.max(jnp.sum(jnp.abs(skew_part), axis=2), axis=1)
    unit_matrix = jnp.eye(gram_matrix.shape[1], dtype=jnp.float32)
    current = unit_matrix[None] + skew_part / row_bound[:, None, None]
    for index in range(newton_turns):
        inner_gram = jnp.einsum("pcd,pce->pde", current, current, precision=highest)
        current = jnp.einsum(
            "pcd,pde->pce", current, 1.5 * unit_matrix[None] - 0.5 * inner_gram, precision=highest
        )
    return current


def full_gram(paired):
    local_gram = jnp.einsum("rpc,rpd->pcd", paired, paired, precision=highest)
    return lax.psum(local_gram, "row")


def assemble(carried, cross_gram):
    first_diag = carried[0::2]
    second = carried[1::2]
    upper_rows = jnp.concatenate([first_diag, cross_gram], axis=2)
    lower_rows = jnp.concatenate([jnp.swapaxes(cross_gram, 1, 2), second], axis=2)
    return jnp.concatenate([upper_rows, lower_rows], axis=1)


def body(snapshot, weights, block_home, plan):
    row_count = snapshot.shape[0]
    block_width = weights.shape[1]
    slot_count = block_home.shape[0]
    rounds = plan.shape[0]
    blocks_here = snapshot.reshape(row_count, slot_count, block_width)
    spread = jnp.take(weights, block_home, axis=0)
    carried = jnp.zeros((slot_count, block_width, block_width), jnp.float32)
    for round_index in range(rounds):
        ordering = plan[round_index, 0]
        blocks_here = jnp.take(blocks_here, ordering, axis=1)
        spread = jnp.take(spread, ordering, axis=0)
        paired = blocks_here.reshape(row_count, 2, 2 * block_width)
        if round_index == 0:
            gram_matrix = full_gram(paired)
        else:
            carried = jnp.take(carried, ordering, axis=0)
            local_cross = jnp.einsum(
                "rpc,rpd->pcd", blocks_here[:, 0::2], blocks_here[:, 1::2], precision=highest
            )
            cross_gram = lax.psum(local_cross, "row")
            gram_matrix = assemble(carried, cross_gram)
        turn_matrix = rotation(gram_matrix, spread.reshape(2, 2 * block_width))
        result = jnp.einsum("rpc,pcd->rpd", paired, turn_matrix, precision=highest)
        blocks_here = result.reshape(row_count, slot_count, block_width)
        gram_times = jnp.einsum("pcd,pde->pce", gram_matrix, turn_matrix, precision=highest)
        rotated_gram = jnp.einsum("pcd,pce->pde", turn_matrix, gram_times, precision=highest)
        carried = jnp.stack(
            [
                rotated_gram[:, :block_width, :block_width],
                rotated_gram[:, block_width:, block_width:],
            ],
            axis=1,
        ).reshape(slot_count, block_width, block_width)
        ahead_block, ahead_scale, ahead_own = shifted(
            (blocks_here[:, 0], spread[0], carried[0]), "pair", 1
        )
        behind_block, behind_scale, behind_own = shifted(
            (blocks_here[:, 3], spread[3], carried[3]), "pair", -1
        )
        carried = jnp.stack([ahead_own, carried[1], carried[2], behind_own], axis=0)
        blocks_here = jnp.stack(
            [ahead_block, blocks_here[:, 1], blocks_here[:, 2], behind_block], axis=1
        )
        spread = jnp.stack([ahead_scale, spread[1], spread[2], behind_scale], axis=0)
    final_matrix = blocks_here.reshape(row_count, slot_count * block_width)
    squares = jnp.diagonal(carried, axis1=1, axis2=2).reshape(slot_count * block_width)
    return (final_matrix, jnp.sqrt(squares))


def solution(mesh):
    in_specs = (P("row", "pair"), P(), P("pair"), P(None, "pair", None))
    out_specs = (P("row", "pair"), P("pair"))
    return jax.shard_map(body, mesh=mesh, in_specs=in_specs, out_specs=out_specs, check_vma=False)
```

profile of v0, /device:TPU:0, one launch (start us, length us, event | category | flops | bytes accessed | tf_op | source)
XLA Modules:
  0.0 318.9 jit_solution(17270181886986516772)
XLA Ops:
  7.9 0.7 compare_and_fusion.1
  8.6 0.7 compare_and_fusion.2
  11.1 1.2 copy.124
  13.5 1.5 fusion.21
  16.5 110.4 %all-reduce.3.cloned.1.call-done = f32[2,256,256]{2,1,0:T(8,128)} async-done(((f32[2,256,256]{2,1,0:T(8,128)}), f32[2,256,256]{2,1,0:T(8,128)}) %all-reduce.3.cloned.1.call-update) | async-done | bytes 524304 | tf_op jit(solution)/shard_map/psum | solution.py:36
  126.9 17.3 %copy.128 = f32[2,256,256]{0,2,1:T(8,128)} copy(f32[2,256,256]{2,1,0:T(8,128)} %all-reduce.3.cloned.1.call-done) | data formatting | bytes 1048576 | tf_op jit(solution)/shard_map/psum | solution.py:36
  144.2 2.3 gather_fusion
  147.1 1.4 fusion.9
  148.5 0.8 fusion.16
  149.3 1.1 fusion.8
  151.1 1.1 fusion.7
  152.8 1.1 fusion.6
  154.6 1.1 fusion.5
  156.3 1.1 fusion.28
  158.1 1.3 fusion.27
  162.8 1.3 fusion.10
  164.4 104.3 %all-reduce.5.cloned.1.call-done = f32[2,128,128]{2,1,0:T(8,128)} async-done(((f32[2,128,128]{2,1,0:T(8,128)}), f32[2,128,128]{2,1,0:T(8,128)}) %all-reduce.5.cloned.1.call-update) | async-done | bytes 131088 | tf_op jit(solution)/shard_map/psum | solution.py:67
  268.7 1.1 copy.144
  269.8 0.9 maximum_maximum_fusion
  270.7 16.6 %copy.145 = f32[2,256,256]{0,2,1:T(8,128)} copy(f32[2,256,256]{2,1,0:T(8,128)S(1)} %maximum_maximum_fusion) | data formatting | bytes 1048576 | tf_op jit(solution)/shard_map/concatenate | solution.py:44
  287.3 2.3 gather_fusion.3
  290.2 1.4 fusion.4
  291.6 0.8 fusion.17
  292.4 1.1 fusion.3
  294.2 1.1 fusion.2
  295.9 1.1 fusion.1
  297.7 1.1 fusion
  299.5 1.1 fusion.33
  301.2 1.1 fusion.34
  303.9 4.6 %copy.159 = f32[4,128,128]{0,2,1:T(8,128)} copy(f32[4,128,128]{2,1,0:T(8,128)S(1)} %pad_maximum_fusion.5) | data formatting | bytes 524288 | tf_op jit(solution)/shard_map/stack | solution.py:87
  308.5 1.8 gather_fusion.4
  311.1 1.0 copy.179
  (106 shorter events, 18.6 us)
Async XLA Ops:
  7.2 2.1 copy-start
  7.2 119.7 %all-reduce.3.cloned.1.call-start = ((), (), s32[]{:S(2)}) async-start(), calls=%async_computation | async-start | bytes 1048576 | tf_op jit(solution)/shard_map/psum | solution.py:36
  10.5 5.2 %collective-permute-start.5 = (f32[128]{0:T(128)S(1)}, f32[128]{0:T(128)S(1)}, u32[]{:S(2)}, u32[]{:S(2)}) collective-permute-start(f32[128]{0:T(128)S(1)} %get-tuple-element.23), channel_id=1, source_target_pairs={{16,0},{0,16},{17,1},{1,17},{18,2},{2,18},{19,3},{3,19},{20,4},{4,... | collective-permute-start | bytes 1544 | tf_op jit(solution)/shard_map/ppermute | solution.py:15
  11.0 4.8 %collective-permute-start.4 = (f32[128]{0:T(128)S(1)}, f32[128]{0:T(128)S(1)}, u32[]{:S(2)}, u32[]{:S(2)}) collective-permute-start(f32[128]{0:T(128)S(1)} %get-tuple-element.22), channel_id=1, source_target_pairs={{16,0},{0,16},{17,1},{1,17},{18,2},{2,18},{19,3},{3,19},{20,4},{4,... | collective-permute-start | bytes 1544 | tf_op jit(solution)/shard_map/ppermute | solution.py:15
  14.9 253.7 %all-reduce.5.cloned.1.call-start = ((), (), s32[]{:S(2)}) async-start(), calls=%async_computation.1 | async-start | bytes 262144 | tf_op jit(solution)/shard_map/psum | solution.py:67
  126.9 19.8 %copy-start.2 = (f32[2,256,256]{2,1,0:T(8,128)S(1)}, f32[2,256,256]{2,1,0:T(8,128)}, u32[]{:S(2)}) copy-start(f32[2,256,256]{2,1,0:T(8,128)} %all-reduce.3.cloned.1.call-done) | copy-start | bytes 1572868
  159.5 1.6 collective-permute-start.1
  159.6 1.5 collective-permute-start
  160.2 1.6 collective-permute-start.3
  160.6 1.5 collective-permute-start.2
  268.7 21.0 %copy-start.3 = (f32[2,128,128]{2,1,0:T(8,128)S(1)}, f32[2,128,128]{2,1,0:T(8,128)}, u32[]{:S(2)}) copy-start(f32[2,128,128]{2,1,0:T(8,128)} %all-reduce.5.cloned.1.call-done) | copy-start | bytes 393220
  269.8 42.3 %copy-start.1 = (f32[8,128]{1,0:T(8,128)S(1)}, f32[8,128]{1,0:T(8,128)}, u32[]{:S(2)}) copy-start(f32[8,128]{1,0:T(8,128)} %param.9) | copy-start | bytes 12292
  302.4 1.3 collective-permute-start.9
  302.5 1.4 collective-permute-start.8
  303.0 8.0 %collective-permute-start.7 = (f32[256,128]{0,1:T(8,128)S(1)}, f32[256,128]{0,1:T(8,128)S(1)}, u32[]{:S(2)}, u32[]{:S(2)}) collective-permute-start(f32[256,128]{0,1:T(8,128)S(1)} %get-tuple-element.11), channel_id=1, source_target_pairs={{16,0},{0,16},{17,1},{1,17},{18,2},{2,18},{19,3},{3,19},{20,4},{4,... | collective-permute-start | bytes 393224 | tf_op jit(solution)/shard_map/ppermute | solution.py:15
  303.2 7.8 %collective-permute-start.6 = (f32[256,128]{0,1:T(8,128)S(1)}, f32[256,128]{0,1:T(8,128)S(1)}, u32[]{:S(2)}, u32[]{:S(2)}) collective-permute-start(f32[256,128]{0,1:T(8,128)S(1)} %get-tuple-element.10), channel_id=1, source_target_pairs={{16,0},{0,16},{17,1},{1,17},{18,2},{2,18},{19,3},{3,19},{20,4},{4,... | collective-permute-start | bytes 393224 | tf_op jit(solution)/shard_map/ppermute | solution.py:15
Sparse Core Ops, SparseCore 0:
  15.1 111.7 all-reduce.2
  164.3 104.3 all-reduce.4
where the time goes:
time: 320 us; the launch traced here: 319 us
  waiting for transfers between devices  215 us (67%)
  local copies, waits for them, and re-layouts  53.7 us (17%)
  matrix products  26.9 us (8%)
  between operations  14.6 us (5%)
  other arithmetic  5.34 us (2%)
    psum x1, waiting for transfers between devices, full_gram(): return lax.psum(local_gram, 'row')  110 us
    psum x1, waiting for transfers between devices, body(): cross_gram = lax.psum(local_cross, 'row')  104 us
    psum x1, local copies, waits for them, and re-layouts, full_gram(): return lax.psum(local_gram, 'row')  17.3 us
    concatenate x1, local copies, waits for them, and re-layouts, assemble(): return jnp.concatenate([upper_rows, lower_rows], axis=1)  16.6 us
    dot_general x10, matrix products, rotation(): inner_gram = jnp.einsum('pcd,pce->pde', current, current, precision=highest)  11.4 us
    dot_general x10, matrix products, rotation(): jnp.einsum('pcd,pde->pce', current, 1.5 * unit_matrix[None] - 0.5 * inner...  6.9 us
  transfers between devices with their start and end apart: 12, of which 5 were waited for; matrix products, arithmetic and copies ran while one was open for 4% of the time, Pallas kernels for 0%

commit v1 on v0

--- a/solution.py
+++ b/solution.py
@@ -64,7 +64,7 @@
             local_cross = jnp.einsum(
                 "rpc,rpd->pcd", blocks_here[:, 0::2], blocks_here[:, 1::2], precision=highest
             )
-            cross_gram = lax.psum(local_cross, "row")
+            cross_gram = jnp.sum(lax.all_gather(local_cross, "row"), axis=0)
             gram_matrix = assemble(carried, cross_gram)
         turn_matrix = rotation(gram_matrix, spread.reshape(2, 2 * block_width))
         result = jnp.einsum("rpc,pcd->rpd", paired, turn_matrix, precision=highest)

time: 320 us -> 270 us (0.84)
  waiting for transfers between devices: 215 us -> 167 us
    psum x1 -> x0, waiting for transfers between devices: 104 us -> none  [body(): cross_gram = lax.psum(local_cross, 'row')]
    all_gather x0 -> x1, waiting for transfers between devices: none -> 53 us  [body(): cross_gram = jnp.sum(lax.all_gather(local_cross, 'row'), axis=0)]
  transfers between devices with their start and end apart: 12 -> 12, of which waited for: 5 -> 10; matrix products, arithmetic and copies ran while one was open for 4% -> 5% of each run, Pallas kernels for 0% -> 0%
where the time goes in v1:
time: 270 us
  waiting for transfers between devices  167 us (62%)
  local copies, waits for them, and re-layouts  52.7 us (20%)
  matrix products  26.7 us (10%)
  between operations  14.6 us (5%)
  other arithmetic  5.48 us (2%)
  starting transfers between devices  3.12 us (1%)
    psum x1, waiting for transfers between devices, full_gram(): return lax.psum(local_gram, 'row')  111 us
    all_gather x1, waiting for transfers between devices, body(): cross_gram = jnp.sum(lax.all_gather(local_cross, 'row'), axis=0)  53 us
    psum x1, local copies, waits for them, and re-layouts, full_gram(): return lax.psum(local_gram, 'row')  17.3 us
    concatenate x1, local copies, waits for them, and re-layouts, assemble(): return jnp.concatenate([upper_rows, lower_rows], axis=1)  16.6 us
    dot_general x10, matrix products, rotation(): inner_gram = jnp.einsum('pcd,pce->pde', current, current, precision=highest)  11.5 us
    dot_general x10, matrix products, rotation(): jnp.einsum('pcd,pde->pce', current, 1.5 * unit_matrix[None] - 0.5 * inner...  6.9 us
  transfers between devices with their start and end apart: 12, of which 10 were waited for; matrix products, arithmetic and copies ran while one was open for 5% of the time, Pallas kernels for 0%

profile of v1, /device:TPU:0, one launch (start us, length us, event | category | flops | bytes accessed | tf_op | source)
XLA Modules:
  0.0 269.6 jit_solution(9353111588366096347)
XLA Ops:
  7.2 0.7 compare_and_fusion.2
  7.9 1.2 copy.124
  10.3 1.5 fusion.21
  11.8 0.7 compare_select_fusion.2
  12.5 0.7 compare_and_fusion.1
  14.5 111.1 %all-reduce.2.cloned.1.call-done = f32[2,256,256]{2,1,0:T(8,128)} async-done(((f32[2,256,256]{2,1,0:T(8,128)}), f32[2,256,256]{2,1,0:T(8,128)}) %all-reduce.2.cloned.1.call-update) | async-done | bytes 524304 | tf_op jit(solution)/shard_map/psum | solution.py:36
  125.6 17.3 %copy.128 = f32[2,256,256]{0,2,1:T(8,128)} copy(f32[2,256,256]{2,1,0:T(8,128)} %all-reduce.2.cloned.1.call-done) | data formatting | bytes 1048576 | tf_op jit(solution)/shard_map/psum | solution.py:36
  142.9 2.3 gather_fusion
  145.8 1.4 fusion.9
  147.2 0.8 fusion.16
  148.0 1.1 fusion.8
  149.8 1.1 fusion.7
  151.6 1.1 fusion.6
  153.3 1.1 fusion.5
  155.1 1.1 fusion.28
  158.7 1.3 fusion.10
  162.9 1.1 fusion.27
  166.6 53.0 %all-gather.3.cloned.1.call-done = f32[32,128,128]{2,1,0:T(8,128)} async-done(((f32[2,128,128]{2,1,0:T(8,128)}), f32[32,128,128]{2,1,0:T(8,128)}) %all-gather.3.cloned.1.call-update) | async-done | bytes 2097168 | tf_op jit(solution)/shard_map/all_gather | solution.py:67
  219.6 1.7 reduce_sum.28
  221.5 16.6 %copy.145 = f32[2,256,256]{0,2,1:T(8,128)} copy(f32[2,256,256]{2,1,0:T(8,128)S(1)} %maximum_maximum_fusion) | data formatting | bytes 1048576 | tf_op jit(solution)/shard_map/concatenate | solution.py:44
  238.0 2.3 gather_fusion.3
  240.9 1.4 fusion.4
  242.3 0.8 fusion.17
  243.2 1.1 fusion.3
  244.9 1.1 fusion.2
  246.7 1.1 fusion.1
  248.4 1.1 fusion
  250.9 1.1 fusion.33
  251.9 1.1 fusion.34
  254.6 4.6 %copy.159 = f32[4,128,128]{0,2,1:T(8,128)} copy(f32[4,128,128]{2,1,0:T(8,128)S(1)} %pad_maximum_fusion.5) | data formatting | bytes 524288 | tf_op jit(solution)/shard_map/stack | solution.py:87
  259.3 1.8 gather_fusion.4
  261.8 1.0 copy.179
  (107 shorter events, 19.8 us)
Async XLA Ops:
  7.2 6.0 %copy-start = (f32[8,128]{1,0:T(8,128)S(1)}, f32[8,128]{1,0:T(8,128)}, u32[]{:S(2)}) copy-start(f32[8,128]{1,0:T(8,128)} %param.9) | copy-start | bytes 12292
  7.2 118.4 %all-reduce.2.cloned.1.call-start = ((), (), s32[]{:S(2)}) async-start(), calls=%async_computation | async-start | bytes 1048576 | tf_op jit(solution)/shard_map/psum | solution.py:36
  10.0 150.8 %copy-start.3 = (s32[2,1,4]{2,1,0:T(1,128)S(1)}, s32[2,1,4]{2,1,0:T(1,128)}, u32[]{:S(2)}) copy-start(s32[2,1,4]{2,1,0:T(1,128)} %param.11) | copy-start | bytes 100
  11.8 207.8 %all-gather.3.cloned.1.call-start = ((), (), s32[]{:S(2)}) async-start(), calls=%async_computation.1 | async-start | bytes 2228224 | tf_op jit(solution)/shard_map/all_gather | solution.py:67
  125.6 19.8 %copy-start.2 = (f32[2,256,256]{2,1,0:T(8,128)S(1)}, f32[2,256,256]{2,1,0:T(8,128)}, u32[]{:S(2)}) copy-start(f32[2,256,256]{2,1,0:T(8,128)} %all-reduce.2.cloned.1.call-done) | copy-start | bytes 1572868
  156.3 1.4 collective-permute-start.3
  156.4 1.5 collective-permute-start.2
  160.1 1.3 collective-permute-start.5
  160.5 1.2 collective-permute-start.4
  164.1 1.3 collective-permute-start.1
  164.4 1.3 collective-permute-start
  221.4 41.4 %copy-start.1 = (f32[8,128]{1,0:T(8,128)S(1)}, f32[8,128]{1,0:T(8,128)}, u32[]{:S(2)}) copy-start(f32[8,128]{1,0:T(8,128)} %param.9) | copy-start | bytes 12292
  253.1 1.3 collective-permute-start.9
  253.2 1.4 collective-permute-start.8
  253.8 8.0 %collective-permute-start.7 = (f32[256,128]{0,1:T(8,128)S(1)}, f32[256,128]{0,1:T(8,128)S(1)}, u32[]{:S(2)}, u32[]{:S(2)}) collective-permute-start(f32[256,128]{0,1:T(8,128)S(1)} %get-tuple-element.11), channel_id=1, source_target_pairs={{16,0},{0,16},{17,1},{1,17},{18,2},{2,18},{19,3},{3,19},{20,4},{4,... | collective-permute-start | bytes 393224 | tf_op jit(solution)/shard_map/ppermute | solution.py:15
  253.9 7.8 %collective-permute-start.6 = (f32[256,128]{0,1:T(8,128)S(1)}, f32[256,128]{0,1:T(8,128)S(1)}, u32[]{:S(2)}, u32[]{:S(2)}) collective-permute-start(f32[256,128]{0,1:T(8,128)S(1)} %get-tuple-element.10), channel_id=1, source_target_pairs={{16,0},{0,16},{17,1},{1,17},{18,2},{2,18},{19,3},{3,19},{20,4},{4,... | collective-permute-start | bytes 393224 | tf_op jit(solution)/shard_map/ppermute | solution.py:15
Sparse Core Ops, SparseCore 0:
  13.7 111.8 all-reduce.1
  160.2 59.3 all-gather.2
